TPU v7x, 32 devices: a whole 2x2x4 slice. The times are simulated.
32 devices in a mesh: rep: 2 (over x), shard: 16 (over z, y, core).
Axes of the slice: x: 2, y: 2, z: 4, core: 2. Of those that a mesh axis runs over, the one named last changes fastest.
Arguments:
- tokens_x: bfloat16 [8192, 4096], P(('rep', 'shard')), may hold values from -6 to 6
- key_grad: bfloat16 [8192, 1024], P(('rep', 'shard')), may hold values from -0.06591797 to 0.06591797
- left_root: bfloat16 [64, 512, 512], P('shard'), may hold values from -1 to 3
- slot_grads: bfloat16 [64, 512, 512], P('shard'), may hold values from -6 to 6
- right_root: bfloat16 [64, 512, 512], P('shard'), may hold values from -1 to 3
- block_slot: int32 [32], replicated, may hold values from 0 to 63, as said below
Outputs:
- grad_key: float32 [4096, 1024], P('shard')
- update: bfloat16 [512, 32, 512], P('shard')
Inputs may be any that keep to these rules, and one draw needn't show every extreme that they name: `block_slot`: the entries are distinct; slot v is slot v % 4 of shard index v // 4; no shard index holds more than 4 blocks, and some shard index holds exactly 4.
All inputs are finite; a program needn't handle non-finite values.
Results may differ from a plain program's by a relative error of at most 0.006.
Values may be sent and summed in bfloat16 or wider, within the bound.
A program may use at most 128 MiB of HBM per device.

v0:
```python
import jax
import jax.numpy as jnp
from jax import lax
from jax.sharding import PartitionSpec as P


def column_term(features, cotangent):
    return lax.dot_general(
        features, cotangent, (((0,), (0,)), ((), ())), preferred_element_type=jnp.float32
    )


def precondition(left_block, grad_block, right_block):
    left_part = jnp.einsum(
        "sij,sjk->sik", left_block, grad_block, preferred_element_type=jnp.float32
    ).astype(jnp.bfloat16)
    return jnp.einsum(
        "sij,sjk->isk", left_part, right_block, preferred_element_type=jnp.float32
    ).astype(jnp.bfloat16)


def shards(tokens_x, key_grad, left_root, slot_grads, right_root, block_slot):
    n_shard = lax.axis_size("shard")
    n_rep = lax.axis_size("rep")
    own_rows = lax.psum_scatter(
        column_term(tokens_x, key_grad), "shard", scatter_dimension=0, tiled=True
    )
    grad_key = lax.psum(own_rows, "rep")
    slot_count = left_root.shape[0]
    half_slots = slot_count // n_rep
    first_slot = lax.axis_index("rep") * half_slots

    def own_half(values):
        return lax.dynamic_slice_in_dim(values, first_slot, half_slots, 0)

    product = precondition(own_half(left_root), own_half(slot_grads), own_half(right_root))
    received = lax.all_to_all(product, "shard", split_axis=0, concat_axis=1, tiled=True)
    joined = lax.all_gather(received, "rep", axis=1, tiled=True)
    owner = block_slot // slot_count
    within = block_slot % slot_count
    position = (
        within // half_slots * (n_shard * half_slots) + owner * half_slots + within % half_slots
    )
    update = jnp.take(joined, position, axis=1)
    return (grad_key, update)


def solution(mesh):
    return jax.shard_map(
        shards,
        mesh=mesh,
        in_specs=(
            P(("rep", "shard"), None),
            P(("rep", "shard"), None),
            P("shard", None, None),
            P("shard", None, None),
            P("shard", None, None),
            P(),
        ),
        out_specs=(P("shard", None), P("shard", None, None)),
        check_vma=False,
    )
```

profile of v0, /device:TPU:0, one launch (start us, length us, event | category | flops | bytes accessed | tf_op | source)
XLA Modules:
  0.0 247.9 jit_solution(18152596970215478150)
XLA Ops:
  8.0 0.0 copy-start
  8.0 0.0 reduce-scatter.2.cloned.1.call-start
  8.1 1.5 copy-done
  9.6 9.2 %fusion.9 = f32[4096,1024]{1,0:T(8,128)} fusion(bf16[256,4096]{1,0:T(8,128)(2,1)S(1)} %copy-done, bf16[256,1024]{1,0:T(8,128)(2,1)} %param.7), kind=kOutput, calls=%fused_computation.23 | convolution fusion | flops 2147483648 | bytes 19398656 | tf_op jit(solution)/shard_map/dot_general | solution.py:8
  18.8 0.0 reduce-scatter.2.cloned.1.call-update
  18.8 0.0 all-gather.2.cloned.1.call-start
  18.8 4.1 %fusion = bf16[512,2,512]{0,2,1:T(8,128)(2,1)} fusion(bf16[4,512,512]{2,1,0:T(8,128)(2,1)} %param.9, s32[]{:T(128)S(6)} %select_n.37, bf16[4,512,512]{2,1,0:T(8,128)(2,1)} %param.8, bf16[4,512,512]{2,1,0:T(8,128)(2,1)} %param.10), kind=kOutput, calls=%fused_computation.3 | convolution fusion | flops 1074790400 | bytes 4195840 | tf_op jit(solution)/shard_map/sij,sjk->isk/dot_general | solution.py:17
  22.9 2.5 %copy.14 = bf16[512,2,512]{2,1,0:T(2,128)(2,1)S(1)} copy(bf16[512,2,512]{0,2,1:T(8,128)(2,1)} %fusion) | data formatting | bytes 2097152 | tf_op jit(solution)/shard_map/convert_element_type | solution.py:19
  25.4 31.9 %all_to_all.18 = bf16[512,2,512]{2,1,0:T(2,128)(2,1)S(1)} all-to-all(bf16[512,2,512]{2,1,0:T(2,128)(2,1)S(1)} %copy.14), channel_id=1, replica_groups=mesh['rep'=2,'shard'=16] {'shard'}, dimensions={0} | all-to-all | bytes 2097152 | tf_op jit(solution)/shard_map/all_to_all | solution.py:37
  57.3 0.2 copy.15
  57.5 0.0 copy-start.1
  57.5 1.0 copy.16
  58.6 0.0 all-gather.2.cloned.1.call-update
  58.6 0.0 all-reduce.2.cloned.1.call-start
  58.6 140.4 %reduce-scatter.2.cloned.1.call-done = f32[256,1024]{1,0:T(8,128)} async-done(((f32[4096,1024]{1,0:T(8,128)}), f32[256,1024]{1,0:T(8,128)}) %reduce-scatter.2.cloned.1.call-update) | async-done | bytes 1048592 | tf_op jit(solution)/shard_map/reduce_scatter | solution.py:25
  199.0 0.0 all-reduce.2.cloned.1.call-update
  199.0 0.0 copy-done.1
  199.1 0.0 all-gather.2.cloned.1.call-done
  199.1 2.2 gather_fusion
  201.3 0.2 select_bitcast_fusion
  201.5 1.5 copy.17
  203.0 35.1 %all-reduce.2.cloned.1.call-done = f32[256,1024]{1,0:T(8,128)} async-done(((f32[256,1024]{1,0:T(8,128)}), f32[256,1024]{1,0:T(8,128)}) %all-reduce.2.cloned.1.call-update) | async-done | bytes 1048592 | tf_op jit(solution)/shard_map/psum | solution.py:28
  238.2 2.3 copy.20
  (2 shorter events, 0.0 us)
Async XLA Ops:
  8.0 1.6 copy-start
  8.0 191.0 %reduce-scatter.2.cloned.1.call-start = ((), (), s32[]{:S(2)}) async-start(), calls=%async_computation.2 | async-start | bytes 17825792 | tf_op jit(solution)/shard_map/reduce_scatter | solution.py:25
  18.8 180.3 %all-gather.2.cloned.1.call-start = ((), (), s32[]{:S(2)}) async-start(), calls=%async_computation.4 | async-start | bytes 3145728 | tf_op jit(solution)/shard_map/all_gather | solution.py:38
  57.5 141.5 %copy-start.1 = (s32[32]{0:T(128)S(1)}, s32[32]{0:T(128)}, u32[]{:S(2)}) copy-start(s32[32]{0:T(128)} %param.11) | copy-start | bytes 388
  58.6 179.6 %all-reduce.2.cloned.1.call-start = ((), (), s32[]{:S(2)}) async-start(), calls=%async_computation.3 | async-start | bytes 2097152 | tf_op jit(solution)/shard_map/psum | solution.py:28
Sparse Core Ops, SparseCore 0:
  18.9 180.0 reduce-scatter.1
Sparse Core Ops, SparseCore 1:
  58.7 33.3 all-gather.1
  199.1 39.0 all-reduce.1
where the time goes:
time: 248 us
  waiting for transfers between devices  176 us (71%)
  blocking collectives  31.9 us (13%)
  between operations  15.6 us (6%)
  matrix products  13.3 us (5%)
  local copies, waits for them, and re-layouts  11.3 us (5%)
    reduce_scatter x1, waiting for transfers between devices, shards(): lax.psum_scatter(column_term(tokens_x, key_grad), 'shard', scatter_dimens...  140 us
    psum x1, waiting for transfers between devices, shards(): grad_key = lax.psum(own_rows, 'rep')  35.1 us
    all_to_all x1, blocking collectives, shards(): lax.all_to_all(product, 'shard', split_axis=0, concat_axis=1, tiled=True)  31.9 us
    dot_general x1, matrix products, column_term(): lax.dot_general(features, cotangent, (((0,), (0,)), ((), ())), preferred_...  9.16 us
    unnamed x6, local copies, waits for them, and re-layouts  5.4 us
  transfers between devices with their start and end apart: 3, of which 2 were waited for; matrix products, arithmetic and copies ran while one was open for 5% of the time, Pallas kernels for 0%

commit v1 on v0

--- a/solution.py
+++ b/solution.py
@@ -25,7 +25,7 @@
     own_rows = lax.psum_scatter(
         column_term(tokens_x, key_grad), "shard", scatter_dimension=0, tiled=True
     )
-    grad_key = lax.psum(own_rows, "rep")
+    grad_key = jnp.sum(lax.all_gather(own_rows, "rep"), axis=0)
     slot_count = left_root.shape[0]
     half_slots = slot_count // n_rep
     first_slot = lax.axis_index("rep") * half_slots

time: 248 us -> 242 us (0.976)
  waiting for transfers between devices: 176 us -> 169 us
  other arithmetic: 0.2 us -> 3.02 us
    psum x1 -> x0, waiting for transfers between devices: 35.1 us -> none  [shards(): grad_key = lax.psum(own_rows, 'rep')]
    all_gather x0 -> x1, waiting for transfers between devices: none -> 28.2 us  [shards(): grad_key = jnp.sum(lax.all_gather(own_rows, 'rep'), axis=0)]
    reduce_sum x0 -> x1, other arithmetic: none -> 2.82 us  [shards(): grad_key = jnp.sum(lax.all_gather(own_rows, 'rep'), axis=0)]
    unnamed x6 -> x5, local copies, waits for them, and re-layouts: 5.4 us -> 3.1 us
where the time goes in v1:
time: 242 us; the launch traced here: 241 us
  waiting for transfers between devices  169 us (70%)
  blocking collectives  31.9 us (13%)
  between operations  15.5 us (6%)
  matrix products  13.3 us (5%)
  local copies, waits for them, and re-layouts  9.02 us (4%)
  other arithmetic  3.02 us (1%)
    reduce_scatter x1, waiting for transfers between devices, shards(): lax.psum_scatter(column_term(tokens_x, key_grad), 'shard', scatter_dimens...  140 us
    all_to_all x1, blocking collectives, shards(): lax.all_to_all(product, 'shard', split_axis=0, concat_axis=1, tiled=True)  31.9 us
    all_gather x1, waiting for transfers between devices, shards(): grad_key = jnp.sum(lax.all_gather(own_rows, 'rep'), axis=0)  28.2 us
    dot_general x1, matrix products, column_term(): lax.dot_general(features, cotangent, (((0,), (0,)), ((), ())), preferred_...  9.16 us
  transfers between devices with their start and end apart: 3, of which 2 were waited for; matrix products, arithmetic and copies ran while one was open for 5% of the time, Pallas kernels for 0%

profile of v1, /device:TPU:0, one launch (start us, length us, event | category | flops | bytes accessed | tf_op | source)
XLA Modules:
  0.0 241.4 jit_solution(8970575319001611127)
XLA Ops:
  8.0 0.0 copy-start
  8.0 0.0 reduce-scatter.2.cloned.1.call-start
  8.1 1.5 copy-done
  9.6 9.2 %fusion.9 = f32[4096,1024]{1,0:T(8,128)} fusion(bf16[256,4096]{1,0:T(8,128)(2,1)S(1)} %copy-done, bf16[256,1024]{1,0:T(8,128)(2,1)} %param.7), kind=kOutput, calls=%fused_computation.23 | convolution fusion | flops 2147483648 | bytes 19398656 | tf_op jit(solution)/shard_map/dot_general | solution.py:8
  18.8 0.0 reduce-scatter.2.cloned.1.call-update
  18.8 0.0 all-gather.4.cloned.1.call-start
  18.8 4.1 %fusion = bf16[512,2,512]{0,2,1:T(8,128)(2,1)} fusion(bf16[4,512,512]{2,1,0:T(8,128)(2,1)} %param.9, s32[]{:T(128)S(6)} %select_n.37, bf16[4,512,512]{2,1,0:T(8,128)(2,1)} %param.8, bf16[4,512,512]{2,1,0:T(8,128)(2,1)} %param.10), kind=kOutput, calls=%fused_computation.3 | convolution fusion | flops 1074790400 | bytes 4195840 | tf_op jit(solution)/shard_map/sij,sjk->isk/dot_general | solution.py:17
  22.9 2.5 %copy.14 = bf16[512,2,512]{2,1,0:T(2,128)(2,1)S(1)} copy(bf16[512,2,512]{0,2,1:T(8,128)(2,1)} %fusion) | data formatting | bytes 2097152 | tf_op jit(solution)/shard_map/convert_element_type | solution.py:19
  25.4 31.9 %all_to_all.18 = bf16[512,2,512]{2,1,0:T(2,128)(2,1)S(1)} all-to-all(bf16[512,2,512]{2,1,0:T(2,128)(2,1)S(1)} %copy.14), channel_id=1, replica_groups=mesh['rep'=2,'shard'=16] {'shard'}, dimensions={0} | all-to-all | bytes 2097152 | tf_op jit(solution)/shard_map/all_to_all | solution.py:37
  57.3 0.2 copy.15
  57.5 0.0 copy-start.1
  57.5 1.0 copy.16
  58.6 0.0 all-gather.4.cloned.1.call-update
  58.6 0.0 all-gather.6.cloned.1.call-start
  58.6 140.4 %reduce-scatter.2.cloned.1.call-done = f32[256,1024]{1,0:T(8,128)} async-done(((f32[4096,1024]{1,0:T(8,128)}), f32[256,1024]{1,0:T(8,128)}) %reduce-scatter.2.cloned.1.call-update) | async-done | bytes 1048592 | tf_op jit(solution)/shard_map/reduce_scatter | solution.py:25
  199.0 0.0 all-gather.6.cloned.1.call-update
  199.0 0.0 copy-done.1
  199.1 0.0 all-gather.4.cloned.1.call-done
  199.1 2.2 gather_fusion
  201.3 0.2 select_bitcast_fusion
  201.5 1.5 copy.17
  203.0 28.2 %all-gather.6.cloned.1.call-done = f32[512,1024]{1,0:T(8,128)} async-done(((f32[256,1024]{1,0:T(8,128)}), f32[512,1024]{1,0:T(8,128)}) %all-gather.6.cloned.1.call-update) | async-done | bytes 2097168 | tf_op jit(solution)/shard_map/all_gather | solution.py:28
  231.2 2.8 %reduce_sum.9 = f32[256,1024]{1,0:T(8,128)} reduce(f32[2,256,1024]{2,1,0:T(8,128)} %bitcast.13, f32[]{:T(128)} %constant.59.clone.1), dimensions={0}, to_apply=%region_1.0 | reduce | flops 262144 | bytes 3145732 | tf_op jit(solution)/shard_map/reduce_sum | solution.py:28
  (2 shorter events, 0.0 us)
Async XLA Ops:
  8.0 1.6 copy-start
  8.0 191.0 %reduce-scatter.2.cloned.1.call-start = ((), (), s32[]{:S(2)}) async-start(), calls=%async_computation.2 | async-start | bytes 17825792 | tf_op jit(solution)/shard_map/reduce_scatter | solution.py:25
  18.8 180.3 %all-gather.4.cloned.1.call-start = ((), (), s32[]{:S(2)}) async-start(), calls=%async_computation.3 | async-start | bytes 3145728 | tf_op jit(solution)/shard_map/all_gather | solution.py:38
  57.5 141.5 %copy-start.1 = (s32[32]{0:T(128)S(1)}, s32[32]{0:T(128)}, u32[]{:S(2)}) copy-start(s32[32]{0:T(128)} %param.11) | copy-start | bytes 388
  58.6 172.6 %all-gather.6.cloned.1.call-start = ((), (), s32[]{:S(2)}) async-start(), calls=%async_computation.4 | async-start | bytes 3145728 | tf_op jit(solution)/shard_map/all_gather | solution.py:28
Sparse Core Ops, SparseCore 0:
  18.9 180.0 reduce-scatter.1
Sparse Core Ops, SparseCore 1:
  58.7 33.3 all-gather.3
  199.1 32.0 all-gather.5
